TPU v7x, 32 devices: a whole 2x2x4 slice. The times are simulated.
32 devices in a mesh: member: 2 (over x), fsdp: 16 (over z, y, core).
Axes of the slice: x: 2, y: 2, z: 4, core: 2. Of those that a mesh axis runs over, the one named last changes fastest.
Arguments:
- latents: bfloat16 [2, 32768, 512], P('member', 'fsdp'), may hold values from -6 to 6
- noise: float32 [2, 32], P('member'), may hold values from -4 to 4
- cond_gain: float32 [32, 512], replicated, may hold values from -0.5 to 0.5
- cond_shift: float32 [32, 512], replicated, may hold values from -0.5 to 0.5
- w_in: bfloat16 [512, 2048], P('fsdp'), may hold values from -0.25 to 0.25
- b_in: float32 [2048], replicated, may hold values from -3 to 3
- w_out: bfloat16 [2048, 512], P('fsdp'), may hold values from -0.125 to 0.125
- target: bfloat16 [32768, 512], P('fsdp'), may hold values from -6 to 6
Outputs:
- prediction: bfloat16 [2, 32768, 512], P('member', 'fsdp')
- grad_in: float32 [512, 2048], P('fsdp')
- grad_out: float32 [2048, 512], P('fsdp')
- crps_mean: float32 [], replicated
All inputs are finite; a program needn't handle non-finite values.
Results may differ from a plain program's by a relative error of at most 0.0043.
Values may be sent and summed in bfloat16 or wider, within the bound.
A program may use at most 128 MiB of HBM per device.

v0:
```python
import jax
import jax.numpy as jnp
from jax import lax
from jax.sharding import PartitionSpec as P

COEF = 0.7978845608
CUBIC = 0.044715


def swapped(block, axis, apart):
    count = lax.axis_size(axis)
    route = []
    for low in range(count):
        high = low | 1 << apart
        if high != low and high < count:
            route += [(low, high), (high, low)]
    return lax.ppermute(block, axis, route)


def gelu_value(v):
    return 0.5 * v * (1.0 + jnp.tanh(COEF * (v + CUBIC * v * v * v)))


def gelu_slope(v):
    u = jnp.tanh(COEF * (v + CUBIC * v * v * v))
    return 0.5 * (1.0 + u) + 0.5 * v * (1.0 - u * u) * COEF * (1.0 + 3.0 * CUBIC * v * v)


def smooth(d):
    return jnp.sqrt(d * d + 0.0625)


def on_device(latents, noise, cond_gain, cond_shift, w_in, b_in, w_out, target):
    block = latents[0]
    noise_row = noise[0]
    rows = block.shape[0]
    width = block.shape[1]
    groups = lax.axis_size("fsdp")
    nodes = rows * groups
    gain = (
        1.0
        + jnp.dot(
            noise_row[None, :],
            cond_gain,
            precision=lax.Precision.HIGHEST,
            preferred_element_type=jnp.float32,
        )[0]
    )
    shift = jnp.dot(
        noise_row[None, :],
        cond_shift,
        precision=lax.Precision.HIGHEST,
        preferred_element_type=jnp.float32,
    )[0]
    values = block.astype(jnp.float32)
    center = jnp.mean(values, axis=1, keepdims=True)
    spread = jnp.mean((values - center) ** 2, axis=1, keepdims=True)
    normed = ((values - center) / jnp.sqrt(spread + 0.25) * gain + shift).astype(jnp.bfloat16)
    columns = normed
    pre = (
        jnp.dot(
            columns,
            lax.all_gather(w_in, "fsdp", axis=0, tiled=True),
            preferred_element_type=jnp.float32,
        )
        + b_in
    )
    act = gelu_value(pre).astype(jnp.bfloat16)
    columns = act
    output = values + jnp.dot(
        columns,
        lax.all_gather(w_out, "fsdp", axis=0, tiled=True),
        preferred_element_type=jnp.float32,
    )
    prediction = output.astype(jnp.bfloat16)
    partner = swapped(prediction, "member", 0)
    mine = prediction.astype(jnp.float32)
    near = mine - target.astype(jnp.float32)
    apart = mine - partner.astype(jnp.float32)
    local_sum = jnp.sum(0.5 * smooth(near) - 0.25 * smooth(apart))
    crps_mean = lax.psum(local_sum, ("member", "fsdp")) / jnp.float32(2 * nodes * width)
    scale = 1.0 / jnp.sqrt(jnp.float32(2 * nodes))
    dpred = ((0.5 * near / smooth(near) - 0.5 * apart / smooth(apart)) * scale).astype(jnp.bfloat16)
    across = (((1,), (1,)), ((), ()))
    dact = lax.dot_general(
        dpred,
        lax.all_gather(w_out, "fsdp", axis=0, tiled=True),
        across,
        preferred_element_type=jnp.float32,
    )
    dpre = (dact * gelu_slope(pre)).astype(jnp.bfloat16)
    contract = (((0,), (0,)), ((), ()))
    columns = normed
    shard_in = lax.psum_scatter(
        lax.dot_general(columns, dpre, contract, preferred_element_type=jnp.float32),
        "fsdp",
        scatter_dimension=0,
        tiled=True,
    )
    columns = act
    shard_out = lax.psum_scatter(
        lax.dot_general(columns, dpred, contract, preferred_element_type=jnp.float32),
        "fsdp",
        scatter_dimension=0,
        tiled=True,
    )
    grad_in, grad_out = lax.psum((shard_in, shard_out), "member")
    return (prediction[None], grad_in, grad_out, crps_mean)


def solution(mesh):
    placed = (
        P("member", "fsdp", None),
        P("member", None),
        P(),
        P(),
        P("fsdp", None),
        P(),
        P("fsdp", None),
        P("fsdp", None),
    )
    return jax.shard_map(
        on_device,
        mesh=mesh,
        in_specs=placed,
        out_specs=(P("member", "fsdp", None), P("fsdp", None), P("fsdp", None), P()),
        check_vma=False,
    )
```

profile of v0, /device:TPU:0, one launch (start us, length us, event | category | flops | bytes accessed | tf_op | source)
XLA Modules:
  0.0 391.8 jit_solution(9791645367214809985)
XLA Ops:
  7.3 0.7 all-gather.3.cloned.1.call-update
  8.0 0.7 all-gather.5.cloned.1.call-update
  8.8 1.9 convert_reduce_fusion
  10.7 0.8 fusion.19
  11.5 2.5 fusion.12
  14.1 0.1 fusion.17
  14.2 40.2 %all-gather.3.cloned.1.call-done = bf16[512,2048]{1,0:T(8,128)(2,1)} async-done(((bf16[32,2048]{1,0:T(8,128)(2,1)}), bf16[512,2048]{1,0:T(8,128)(2,1)}) %all-gather.3.cloned.1.call-update) | async-done | bytes 2097168 | tf_op jit(solution)/shard_map/all_gather | solution.py:63
  54.4 13.9 %multiply_convert_fusion = (bf16[2048,2048]{1,0:T(8,128)(2,1)}, f32[2048,2048]{1,0:T(8,128)}) fusion(f32[2048]{0:T(1024)S(1)} %copy-done.7, bf16[512,2048]{1,0:T(8,128)(2,1)} %all-gather.3.cloned.1.call-done, bf16[1,2048,512]{2,1,0:T(8,128)(2,1)S(1)} %copy-done.1, f32[512]{0:T(512)S(1)} %bitcast.43, f32[512]{0:T(512)S(1)} %broadcast_add_fusion, ...), kind=kOutput, calls=%fused_computation.9 | convolution fusion | flops 4343201792 | bytes 29388800 | tf_op jit(solution)/shard_map/dot_general | solution.py:61
  68.3 28.5 %all-gather.5.cloned.1.call-done = bf16[2048,512]{1,0:T(8,128)(2,1)} async-done(((bf16[128,512]{1,0:T(8,128)(2,1)}), bf16[2048,512]{1,0:T(8,128)(2,1)}) %all-gather.5.cloned.1.call-update) | async-done | bytes 2097168 | tf_op jit(solution)/shard_map/all_gather | solution.py:72
  96.8 8.5 %fusion.16 = bf16[2048,512]{1,0:T(8,128)(2,1)S(1)} fusion(bf16[1,2048,512]{2,1,0:T(8,128)(2,1)S(1)} %copy-done.1, bf16[2048,2048]{1,0:T(8,128)(2,1)} %get-tuple-element.6, bf16[2048,512]{1,0:T(8,128)(2,1)} %all-gather.5.cloned.1.call-done), kind=kOutput, calls=%fused_computation.23 | convolution fusion | flops 4298113024 | bytes 14680064 | tf_op jit(solution)/shard_map/dot_general | solution.py:70
  105.3 1.3 copy-done.3
  106.6 1.5 collective-permute-start
  108.1 46.3 %collective-permute-done = bf16[2048,512]{1,0:T(8,128)(2,1)S(1)} collective-permute-done((bf16[2048,512]{1,0:T(8,128)(2,1)S(1)}, bf16[2048,512]{1,0:T(8,128)(2,1)S(1)}, u32[]{:S(2)}, u32[]{:S(2)}) %collective-permute-start) | collective-permute-done | bytes 2097184 | tf_op jit(solution)/shard_map/ppermute | solution.py:17
  154.4 1.3 copy-done.4
  155.7 30.2 %fusion.7 = f32[512,2048]{1,0:T(8,128)} fusion(f32[2048,2048]{1,0:T(8,128)} %get-tuple-element.7, bf16[2048,512]{1,0:T(8,128)(2,1)} %all-gather.5.cloned.1.call-done, f32[2048]{0:T(1024)S(1)} %copy-done.7, bf16[1,2048,512]{2,1,0:T(8,128)(2,1)S(1)} %copy-done.1, f32[512]{0:T(512)S(1)} %bitcast.44, f32[512]{0:T(512)S(1)} %broadcast_add_fusion, ...), kind=kOutput, calls=%fused_computation.10 | convolution fusion | flops 8696889344 | bytes 31485952 | tf_op jit(solution)/shard_map/dot_general | solution.py:95
  185.9 0.3 reduce-scatter.5.cloned.1.call-start
  186.2 1.3 copy-done.2
  187.5 14.5 %fusion.29 = f32[2048,512]{1,0:T(8,128)} fusion(bf16[2048,2048]{1,0:T(8,128)(2,1)} %get-tuple-element.6, bf16[2048,512]{1,0:T(8,128)(2,1)S(1)} %copy-done.2, bf16[2048,512]{1,0:T(8,128)(2,1)} %copy-done.3, bf16[2048,512]{1,0:T(8,128)(2,1)} %copy-done.4), kind=kOutput, calls=%fused_computation.41 | convolution fusion | flops 4311744512 | bytes 18874368 | tf_op jit(solution)/shard_map/dot_general | solution.py:102
  202.0 55.6 %reduce-scatter.3.cloned.1.call-done = f32[32,2048]{1,0:T(8,128)} async-done(((f32[512,2048]{1,0:T(8,128)}), f32[32,2048]{1,0:T(8,128)}) %reduce-scatter.3.cloned.1.call-update) | async-done | bytes 262160 | tf_op jit(solution)/shard_map/reduce_scatter | solution.py:94
  257.7 75.5 %reduce-scatter.5.cloned.1.call-done = f32[128,512]{1,0:T(8,128)} async-done(((f32[2048,512]{1,0:T(8,128)}), f32[128,512]{1,0:T(8,128)}) %reduce-scatter.5.cloned.1.call-update) | async-done | bytes 262160 | tf_op jit(solution)/shard_map/reduce_scatter | solution.py:101
  333.2 6.5 %subtract_reduce_fusion = f32[]{:T(128)} fusion(bf16[2048,512]{1,0:T(8,128)(2,1)S(1)} %copy-done.2, bf16[2048,512]{1,0:T(8,128)(2,1)} %copy-done.3, bf16[2048,512]{1,0:T(8,128)(2,1)} %copy-done.4), kind=kLoop, calls=%fused_computation.24 | loop fusion | flops 13631487 | bytes 6291460 | tf_op jit(solution)/shard_map/reduce_sum | solution.py:80
  339.7 39.9 %psum.23 = f32[]{:T(128)} all-reduce(f32[]{:T(128)} %subtract_reduce_fusion), channel_id=1, replica_groups=mesh['member'=2,'fsdp'=16] {'member','fsdp'}, use_global_device_ids=true, to_apply=%region_7.0 | all-reduce | flops 1 | bytes 8 | tf_op jit(solution)/shard_map/psum | solution.py:81
  380.3 1.7 copy.14
  382.0 1.7 copy.15
  (24 shorter events, 0.3 us)
Async XLA Ops:
  7.2 3.5 copy-start
  7.2 47.2 %copy-start.1 = (bf16[1,2048,512]{2,1,0:T(8,128)(2,1)S(1)}, bf16[1,2048,512]{2,1,0:T(8,128)(2,1)}, u32[]{:S(2)}) copy-start(bf16[1,2048,512]{2,1,0:T(8,128)(2,1)} %param.8) | copy-start | bytes 6291460
  7.2 6.9 %copy-start.6 = (f32[1,32]{1,0:T(1,128)S(1)}, f32[1,32]{1,0:T(1,128)}, u32[]{:S(2)}) copy-start(f32[1,32]{1,0:T(1,128)} %param.9) | copy-start | bytes 388
  7.2 6.8 %copy-start.5 = (f32[32,512]{1,0:T(8,128)S(1)}, f32[32,512]{1,0:T(8,128)}, u32[]{:S(2)}) copy-start(f32[32,512]{1,0:T(8,128)} %param.11) | copy-start | bytes 196612
  7.2 47.2 %copy-start.7 = (f32[2048]{0:T(1024)S(1)}, f32[2048]{0:T(1024)}, u32[]{:S(2)}) copy-start(f32[2048]{0:T(1024)} %param.13) | copy-start | bytes 24580
  7.2 47.2 %all-gather.3.cloned.1.call-start = ((), (), s32[]{:S(2)}) async-start(), calls=%async_computation.2 | async-start | bytes 2228224 | tf_op jit(solution)/shard_map/all_gather | solution.py:63
  8.0 88.8 %all-gather.5.cloned.1.call-start = ((), (), s32[]{:S(2)}) async-start(), calls=%async_computation.3 | async-start | bytes 2228224 | tf_op jit(solution)/shard_map/all_gather | solution.py:72
  8.7 249.0 %reduce-scatter.3.cloned.1.call-start = ((), (), s32[]{:S(2)}) async-start(), calls=%async_computation.4 | async-start | bytes 4456448 | tf_op jit(solution)/shard_map/reduce_scatter | solution.py:94
  105.3 1.3 copy-start.3
  106.6 47.8 %collective-permute-start = (bf16[2048,512]{1,0:T(8,128)(2,1)S(1)}, bf16[2048,512]{1,0:T(8,128)(2,1)S(1)}, u32[]{:S(2)}, u32[]{:S(2)}) collective-permute-start(bf16[2048,512]{1,0:T(8,128)(2,1)S(1)} %fusion.16), channel_id=1, source_target_pairs={{0,16},{16,0},{1,17},{17,1},{2,18},{18,2},{3,19},{19,3},{4,20},{20... | collective-permute-start | bytes 6291464 | tf_op jit(solution)/shard_map/ppermute | solution.py:17
  154.4 1.3 copy-start.4
  185.9 1.6 copy-start.2
  185.9 147.3 %reduce-scatter.5.cloned.1.call-start = ((), (), s32[]{:S(2)}) async-start(), calls=%async_computation.5 | async-start | bytes 4456448 | tf_op jit(solution)/shard_map/reduce_scatter | solution.py:101
  202.0 178.3 %all-reduce.3.cloned.1.call-start = ((), (), s32[]{:S(2)}) async-start(), calls=%async_computation.6 | async-start | bytes 1048576 | tf_op jit(solution)/shard_map/psum | solution.py:107
Sparse Core Ops, SparseCore 0:
  10.2 44.1 all-gather.2
  56.6 40.1 all-gather.4
  186.0 71.6 reduce-scatter.2
  261.4 71.7 reduce-scatter.4
  335.4 28.1 all-reduce.2
where the time goes:
time: 395 us; the launch traced here: 392 us
  waiting for transfers between devices  248 us (63%)
  matrix products  68 us (17%)
  blocking collectives  39.9 us (10%)
  between operations  16.1 us (4%)
  other arithmetic  10.9 us (3%)
  local copies, waits for them, and re-layouts  7.28 us (2%)
    reduce_scatter x1, waiting for transfers between devices, on_device(): lax.psum_scatter(lax.dot_general(columns, dpred, contract, preferred_elem...  75.5 us
    reduce_scatter x1, waiting for transfers between devices, on_device(): lax.psum_scatter(lax.dot_general(columns, dpre, contract, preferred_eleme...  55.6 us
    ppermute x1, waiting for transfers between devices, swapped(): return lax.ppermute(block, axis, route)  46.3 us
    all_gather x1, waiting for transfers between devices, on_device(): lax.all_gather(w_in, 'fsdp', axis=0, tiled=True)  40.2 us
    psum x1, blocking collectives, on_device(): lax.psum(local_sum, ('member', 'fsdp')) / jnp.float32(2 * nodes * width)  39.9 us
    dot_general x1, matrix products, on_device(): lax.dot_general(columns, dpre, contract, preferred_element_type=jnp.float32)  30.2 us
    all_gather x1, waiting for transfers between devices, on_device(): lax.all_gather(w_out, 'fsdp', axis=0, tiled=True)  28.5 us
    dot_general x1, matrix products, on_device(): lax.dot_general(columns, dpred, contract, preferred_element_type=jnp.floa...  14.5 us
  transfers between devices with their start and end apart: 6, of which 5 were waited for; matrix products, arithmetic and copies ran while one was open for 10% of the time, Pallas kernels for 0%

commit v1 on v0

--- a/solution.py
+++ b/solution.py
@@ -1,6 +1,10 @@
+import functools
+
 import jax
 import jax.numpy as jnp
 from jax import lax
+from jax.experimental import pallas as pl
+from jax.experimental.pallas import tpu as pltpu
 from jax.sharding import PartitionSpec as P
 
 COEF = 0.7978845608
@@ -30,7 +34,7 @@
     return jnp.sqrt(d * d + 0.0625)
 
 
-def on_device(latents, noise, cond_gain, cond_shift, w_in, b_in, w_out, target):
+def general(latents, noise, cond_gain, cond_shift, w_in, b_in, w_out, target):
     block = latents[0]
     noise_row = noise[0]
     rows = block.shape[0]
@@ -108,6 +112,408 @@
     return (prediction[None], grad_in, grad_out, crps_mean)
 
 
+TILE = 256
+WIDE = 512
+MESH = pl.DeviceIdType.MESH
+
+
+def fused_kernel(
+    n, gs_in, lat, b_in, w_in, w_out, target,
+    pred, gin, gout, crps,
+    win_s, wout_s, x_s, t_s, gs_s, p_s, norm_t, norm_s, act_s, slope_s, dp_s, dp_t, dpre_s, cr_s,
+    pair_tx, pair_rx, ring_tx, ring_rx, mine_s, gin_tx, gout_tx, gin_rx, gout_rx, cr_tx, cr_rx,
+    g_send, g_recv, q_send, q_recv, l_send, l_recv, local_sem, p_send, p_recv, o_sem,
+    pair_ss, pair_rs, ring_ss, ring_rs, fin_ss, fin_rs, out_ss, out_rs, cr_ss, cr_rs,
+):
+    m = lax.axis_index("member")
+    f = lax.axis_index("fsdp")
+    chips = n // 2
+    core = f % 2
+    chip = f // 2
+    turn = 1 - 2 * core
+
+    def chip_at(place):
+        low = place < chips // 2
+        return jnp.where(low, 2 * place, 2 * (chips - 1 - place) + 1)
+
+    position = jnp.where(chip % 2 == 0, chip // 2, chips - 1 - chip // 2)
+
+    def place(offset):
+        return (position + turn * offset + 2 * chips) % chips
+
+    following = (m, 2 * chip_at(place(1)) + core)
+    twin = (m, 2 * chip + 1 - core)
+    partner = (1 - m, f)
+    flat = m * n + f
+    total = 2 * n
+
+    def device(index):
+        return (index // n, index % n)
+
+    barrier = pltpu.get_barrier_semaphore()
+
+    @pl.loop(1, total)
+    def greet(k):
+        pl.semaphore_signal(barrier, inc=1, device_id=device((flat + k) % total), device_id_type=MESH)
+
+    pl.semaphore_wait(barrier, total - 1)
+
+    def remote(src, dst, send, recv, to):
+        return pltpu.make_async_remote_copy(
+            src_ref=src, dst_ref=dst, send_sem=send, recv_sem=recv, device_id=to, device_id_type=MESH
+        )
+
+    half = x_s.shape[1]
+    width = x_s.shape[2]
+    hidden = win_s.shape[1]
+    rin = w_in.shape[0]
+    rout = w_out.shape[0]
+    mine_from = pl.multiple_of(m * half, half)
+    other_from = pl.multiple_of((1 - m) * half, half)
+
+    def slot(which, owner):
+        if which == 0:
+            return win_s.at[pl.ds(pl.multiple_of(owner * rin, rin), rin)]
+        return wout_s.at[pl.ds(pl.multiple_of(owner * rout, rout), rout)]
+
+    def ring_copy(which, step, src, owner):
+        return remote(src, slot(which, owner), g_send.at[which, step], g_recv.at[which, step], following)
+
+    def pair_copy(which, step, src, owner):
+        return remote(src, slot(which, owner), q_send.at[which, step], q_recv.at[which, step], twin)
+
+    shards = (w_in, w_out)
+    for which in range(2):
+        ring_copy(which, 0, shards[which], f).start()
+    swap = remote(lat.at[pl.ds(other_from, half)], x_s.at[0], l_send.at[0], l_recv.at[0], partner)
+    swap.start()
+    gs_swap = remote(gs_in, gs_s.at[0], l_send.at[1], l_recv.at[1], partner)
+    gs_swap.start()
+    for which in range(2):
+        pair_copy(which, 0, shards[which], f).start()
+    keep = pltpu.make_async_copy(lat.at[pl.ds(mine_from, half)], x_s.at[1], local_sem.at[0])
+    keep.start()
+    goal = pltpu.make_async_copy(target.at[pl.ds(mine_from, half)], t_s, local_sem.at[1])
+    goal.start()
+    gs_s[1] = gs_in[...]
+    cr_s[...] = jnp.zeros_like(cr_s)
+    win_s[pl.ds(pl.multiple_of(f * rin, rin), rin), :] = w_in[...]
+    wout_s[pl.ds(pl.multiple_of(f * rout, rout), rout), :] = w_out[...]
+
+    for step in range(1, chips):
+        owner = 2 * chip_at(place(-step)) + core
+        for which in range(2):
+            ring_copy(which, step - 1, slot(which, owner), owner).wait_recv()
+            if step < chips - 1:
+                ring_copy(which, step, slot(which, owner), owner).start()
+            pair_copy(which, step, slot(which, owner), owner).start()
+    for step in range(chips):
+        owner = 2 * chip_at(place(step)) + 1 - core
+        for which in range(2):
+            pair_copy(which, step, slot(which, owner), owner).wait_recv()
+    for step in range(chips):
+        owner = 2 * chip_at(place(-step)) + core
+        for which in range(2):
+            src = shards[which] if step == 0 else slot(which, owner)
+            if step < chips - 1:
+                ring_copy(which, step, src, owner).wait_send()
+            pair_copy(which, step, src, owner).wait_send()
+    keep.wait()
+    goal.wait()
+    gs_swap.wait()
+    swap.wait()
+
+    tiles = half // TILE
+    scale = (1.0 / (2.0 * n * 2 * half) ** 0.5)
+
+    def home(tile):
+        start = pl.multiple_of(tile * TILE, TILE)
+        there = pl.multiple_of(m * half + tile * TILE, TILE)
+        back = remote(p_s.at[0, pl.ds(start, TILE)], pred.at[pl.ds(there, TILE)], p_send.at[tile], p_recv.at[tile], partner)
+        here = pltpu.make_async_copy(p_s.at[1, pl.ds(start, TILE)], pred.at[pl.ds(there, TILE)], o_sem.at[tile])
+        return back, here
+
+    def arrival(tile):
+        start = pl.multiple_of(tile * TILE, TILE)
+        there = pl.multiple_of((1 - m) * half + tile * TILE, TILE)
+        return remote(p_s.at[0, pl.ds(start, TILE)], pred.at[pl.ds(there, TILE)], p_send.at[tile], p_recv.at[tile], partner)
+
+    @pl.loop(0, tiles)
+    def nodes(tile):
+        start = pl.multiple_of(tile * TILE, TILE)
+        base = pl.multiple_of(tile * 2 * TILE, 2 * TILE)
+        rows = pl.ds(base, 2 * TILE)
+        for side in range(2):
+            values = x_s[side, pl.ds(start, TILE), :].astype(jnp.float32)
+            center = jnp.mean(values, axis=1, keepdims=True)
+            moved = values - center
+            spread = jnp.mean(moved * moved, axis=1, keepdims=True)
+            normed = moved * lax.rsqrt(spread + 0.25) * gs_s[side, 0:1, :] + gs_s[side, 1:2, :]
+            normed = normed.astype(jnp.bfloat16)
+            norm_s[side * TILE : (side + 1) * TILE, :] = normed
+        norm_t[:, rows] = norm_s[...].T
+        for j in range(hidden // WIDE):
+            cols = slice(j * WIDE, (j + 1) * WIDE)
+            v = jnp.dot(norm_s[...], win_s[:, cols], preferred_element_type=jnp.float32) + b_in[:, cols]
+            square = v * v
+            u = jnp.tanh(COEF * (v + CUBIC * square * v))
+            gate = 0.5 * (1.0 + u)
+            act_s[rows, cols] = (v * gate).astype(jnp.bfloat16)
+            slope_s[:, cols] = gate + (0.5 * COEF) * v * (1.0 - u * u) * (1.0 + 3.0 * CUBIC * square)
+        out = jnp.dot(act_s[rows, :], wout_s[...], preferred_element_type=jnp.float32)
+        guess = []
+        for side in range(2):
+            value = x_s[side, pl.ds(start, TILE), :].astype(jnp.float32) + out[side * TILE : (side + 1) * TILE]
+            value = value.astype(jnp.bfloat16)
+            p_s[side, pl.ds(start, TILE), :] = value
+            guess.append(value.astype(jnp.float32))
+        goal_tile = t_s[pl.ds(start, TILE), :].astype(jnp.float32)
+        slopes = []
+        value_sum = None
+        for d, weight in ((guess[0] - goal_tile, 0.5), (guess[1] - goal_tile, 0.5), (guess[0] - guess[1], -0.5)):
+            q = d * d + 0.0625
+            r = lax.rsqrt(q)
+            slopes.append(0.5 * d * r)
+            term = weight * (q * r)
+            value_sum = term if value_sum is None else value_sum + term
+        cr_s[...] += jnp.sum(value_sum.reshape(TILE // 8, 8, width), axis=0)
+        dp_s[:TILE, :] = ((slopes[0] - slopes[2]) * scale).astype(jnp.bfloat16)
+        dp_s[TILE:, :] = ((slopes[1] + slopes[2]) * scale).astype(jnp.bfloat16)
+        dp_t[:, rows] = dp_s[...].T
+        for j in range(hidden // WIDE):
+            cols = slice(j * WIDE, (j + 1) * WIDE)
+            dact = lax.dot_general(
+                dp_s[...], wout_s[cols, :], (((1,), (1,)), ((), ())), preferred_element_type=jnp.float32
+            )
+            dpre_s[rows, cols] = (dact * slope_s[:, cols]).astype(jnp.bfloat16)
+        back, here = home(tile)
+        back.start()
+        here.start()
+
+    part = cr_s[:, 0:128]
+    for j in range(1, width // 128):
+        part = part + cr_s[:, j * 128 : (j + 1) * 128]
+    cr_tx[...] = part
+    cr_rx[flat] = part
+
+    def cr_copy(to, source):
+        return remote(cr_tx, cr_rx.at[source], cr_ss.at[to], cr_rs.at[source], device(to))
+
+    cw = hidden // n
+
+    def columns(owner):
+        return pl.ds(pl.multiple_of(owner * cw, cw), cw)
+
+    def pair_sum(which, step):
+        return remote(
+            pair_tx.at[step, which], pair_rx.at[step, which], pair_ss.at[step, which], pair_rs.at[step, which], twin
+        )
+
+    def ring_sum(which, step):
+        return remote(
+            ring_tx.at[step, which], ring_rx.at[step, which], ring_ss.at[step, which], ring_rs.at[step, which], following
+        )
+
+    def compute(step):
+        own = columns(2 * chip_at(place(-step - 1)) + core)
+        twins = columns(2 * chip_at(place(step + 1)) + 1 - core)
+        for which, (left, right) in enumerate(((norm_t, dpre_s), (dp_t, act_s))):
+            both = jnp.concatenate([right[:, own], right[:, twins]], axis=1)
+            product = jnp.dot(left[...], both, preferred_element_type=jnp.float32)
+            mine_s[step, which] = product[:, :cw]
+            pair_tx[step, which] = product[:, cw:].astype(jnp.bfloat16)
+        for which in range(2):
+            pair_sum(which, step).start()
+
+    def finish(step, first=False, last=False):
+        for which in range(2):
+            pair_sum(which, step).wait_recv()
+            value = mine_s[step, which] + pair_rx[step, which].astype(jnp.float32)
+            if not first:
+                ring_sum(which, step - 1).wait_recv()
+                value = value + ring_rx[step - 1, which].astype(jnp.float32)
+            value = value.astype(jnp.bfloat16)
+            if not last:
+                ring_tx[step, which] = value
+                ring_sum(which, step).start()
+            elif which == 0:
+                gin_tx[...] = value
+            else:
+                gout_tx[...] = value
+
+    compute(0)
+    compute(1)
+    finish(0, first=True)
+
+    @pl.loop(1, chips - 1)
+    def steps(step):
+        compute(step + 1)
+        finish(step)
+
+    @pl.loop(1, total)
+    def tell(k):
+        cr_copy((flat + k) % total, flat).start()
+
+    finish(chips - 1, last=True)
+
+    def fin_copy(to, source):
+        target_rows = pl.ds(pl.multiple_of((to % n) * rin, rin), rin)
+        return remote(gin_tx.at[target_rows], gin_rx.at[source], fin_ss.at[to], fin_rs.at[source], device(to))
+
+    out_copy = remote(gout_tx, gout_rx, out_ss, out_rs, partner)
+    out_copy.start()
+
+    @pl.loop(1, total)
+    def scatter(k):
+        fin_copy((flat + k) % total, flat).start()
+
+    gin_rx[flat] = gin_tx[pl.ds(pl.multiple_of(f * rin, rin), rin), :]
+
+    @pl.loop(1, total)
+    def heard(k):
+        cr_copy(flat, (flat + k) % total).wait_recv()
+
+    crps[...] = jnp.sum(cr_rx[...], axis=0)
+
+    out_copy.wait_recv()
+    gout[...] = (gout_tx[...].astype(jnp.float32) + gout_rx[...].astype(jnp.float32)).T
+
+    @pl.loop(1, total)
+    def collect(k):
+        fin_copy(flat, (flat + k) % total).wait_recv()
+
+    for owner in range(n):
+        gin[:, owner * cw : (owner + 1) * cw] = gin_rx[owner].astype(jnp.float32) + gin_rx[n + owner].astype(jnp.float32)
+
+    @pl.loop(0, tiles)
+    def settle(tile):
+        back, here = home(tile)
+        back.wait_send()
+        here.wait()
+        arrival(tile).wait_recv()
+
+    @pl.loop(0, chips - 1)
+    def settle_ring(step):
+        for which in range(2):
+            ring_sum(which, step).wait_send()
+
+    @pl.loop(0, chips)
+    def settle_pair(step):
+        for which in range(2):
+            pair_sum(which, step).wait_send()
+
+    out_copy.wait_send()
+
+    @pl.loop(1, total)
+    def settle_rest(k):
+        to = (flat + k) % total
+        cr_copy(to, flat).wait_send()
+        fin_copy(to, flat).wait_send()
+
+
+def fits(rows, width, hidden, n):
+    return (
+        n >= 4
+        and n % 4 == 0
+        and hidden % n == 0
+        and (hidden // n) % 128 == 0
+        and width % n == 0
+        and (width // n) % 16 == 0
+        and width % 128 == 0
+        and hidden % WIDE == 0
+        and rows % (2 * TILE) == 0
+        and rows * hidden <= 2048 * 2048
+        and width * hidden <= 512 * 2048
+    )
+
+
+def fused(latents, noise, cond_gain, cond_shift, w_in, b_in, w_out, target):
+    block = latents[0]
+    rows, width = block.shape
+    n = lax.axis_size("fsdp")
+    hidden = w_in.shape[1]
+    half = rows // 2
+    chips = n // 2
+    tiles = half // TILE
+    cw = hidden // n
+    rin, rout = w_in.shape[0], w_out.shape[0]
+    exact = functools.partial(jnp.dot, precision=lax.Precision.HIGHEST, preferred_element_type=jnp.float32)
+    gs = jnp.concatenate([1.0 + exact(noise, cond_gain), exact(noise, cond_shift), jnp.zeros((6, width), jnp.float32)])
+    bf, f32 = jnp.bfloat16, jnp.float32
+    vmem = pl.BlockSpec(memory_space=pltpu.VMEM)
+    anywhere = pl.BlockSpec(memory_space=pl.ANY)
+    dma = pltpu.SemaphoreType.DMA
+    prediction, grad_in, grad_out, parts = pl.pallas_call(
+        functools.partial(fused_kernel, n),
+        out_shape=(
+            jax.ShapeDtypeStruct((rows, width), bf),
+            jax.ShapeDtypeStruct((rin, hidden), f32),
+            jax.ShapeDtypeStruct((rout, width), f32),
+            jax.ShapeDtypeStruct((8, 128), f32),
+        ),
+        in_specs=[vmem, anywhere, vmem, vmem, vmem, anywhere],
+        out_specs=(anywhere, vmem, vmem, vmem),
+        scratch_shapes=[
+            pltpu.VMEM((width, hidden), bf),
+            pltpu.VMEM((hidden, width), bf),
+            pltpu.VMEM((2, half, width), bf),
+            pltpu.VMEM((half, width), bf),
+            pltpu.VMEM((2, 8, width), f32),
+            pltpu.VMEM((2, half, width), bf),
+            pltpu.VMEM((width, rows), bf),
+            pltpu.VMEM((2 * TILE, width), bf),
+            pltpu.VMEM((rows, hidden), bf),
+            pltpu.VMEM((2 * TILE, hidden), f32),
+            pltpu.VMEM((2 * TILE, width), bf),
+            pltpu.VMEM((width, rows), bf),
+            pltpu.VMEM((rows, hidden), bf),
+            pltpu.VMEM((8, width), f32),
+            pltpu.VMEM((chips, 2, width, cw), bf),
+            pltpu.VMEM((chips, 2, width, cw), bf),
+            pltpu.VMEM((chips - 1, 2, width, cw), bf),
+            pltpu.VMEM((chips - 1, 2, width, cw), bf),
+            pltpu.VMEM((chips, 2, width, cw), f32),
+            pltpu.VMEM((width, cw), bf),
+            pltpu.VMEM((width, cw), bf),
+            pltpu.VMEM((2 * n, rin, cw), bf),
+            pltpu.VMEM((width, cw), bf),
+            pltpu.VMEM((8, 128), f32),
+            pltpu.VMEM((2 * n, 8, 128), f32),
+            dma((2, chips)),
+            dma((2, chips)),
+            dma((2, chips)),
+            dma((2, chips)),
+            dma((2,)),
+            dma((2,)),
+            dma((2,)),
+            dma((tiles,)),
+            dma((tiles,)),
+            dma((tiles,)),
+            dma((chips, 2)),
+            dma((chips, 2)),
+            dma((chips, 2)),
+            dma((chips, 2)),
+            dma((2 * n,)),
+            dma((2 * n,)),
+            dma,
+            dma,
+            dma((2 * n,)),
+            dma((2 * n,)),
+        ],
+        compiler_params=pltpu.CompilerParams(
+            collective_id=0, has_side_effects=True, vmem_limit_bytes=60 * 1024 * 1024
+        ),
+    )(gs, block, b_in[None, :], w_in, w_out, target)
+    crps_mean = jnp.sum(parts) / jnp.float32(2 * rows * n * width)
+    return (prediction[None], grad_in, grad_out, crps_mean)
+
+
+def on_device(latents, noise, cond_gain, cond_shift, w_in, b_in, w_out, target):
+    n = lax.axis_size("fsdp")
+    form = fused if fits(latents.shape[1], latents.shape[2], w_in.shape[1], n) else general
+    return form(latents, noise, cond_gain, cond_shift, w_in, b_in, w_out, target)
+
+
 def solution(mesh):
     placed = (
         P("member", "fsdp", None),

time: 395 us -> 115 us (0.29)
  waiting for transfers between devices: 248 us -> 0 us
  Pallas kernels: 0 us -> 103 us
  matrix products: 68 us -> 1.81 us
  blocking collectives: 39.9 us -> 0 us
  between operations: 16.1 us -> 2.47 us
  other arithmetic: 10.9 us -> 1.98 us
    reduce_scatter x2 -> x0, waiting for transfers between devices: 131 us -> none  [the longest x1 75.5 us: on_device(): lax.psum_scatter(lax.dot_general(columns, dpred, contract, preferred_elem...]
    pallas_call x0 -> x1, Pallas kernels: none -> 103 us  [fused(): pl.pallas_call(functools.partial(fused_kernel, n), out_shape=(jax.ShapeDt...]
    all_gather x2 -> x0, waiting for transfers between devices: 68.7 us -> none  [the longest x1 40.2 us: on_device(): lax.all_gather(w_in, 'fsdp', axis=0, tiled=True)]
    dot_general x6 -> x2, matrix products: 68 us -> 1.81 us  [the longest x1 1.01 us: fused(): exact(noise, cond_shift)]
    ppermute x1 -> x0, waiting for transfers between devices: 46.3 us -> none  [swapped(): return lax.ppermute(block, axis, route)]
    psum x1 -> x0, blocking collectives: 39.9 us -> none  [on_device(): lax.psum(local_sum, ('member', 'fsdp')) / jnp.float32(2 * nodes * width)]
    reduce_sum x3 -> x1, other arithmetic: 10.9 us -> 1.29 us  [fused(): crps_mean = jnp.sum(parts) / jnp.float32(2 * rows * n * width)]
  transfers between devices with their start and end apart: 6 -> 0, of which waited for: 5 -> 0; matrix products, arithmetic and copies ran while one was open for 10% -> 0% of each run, Pallas kernels for 0% -> 0%
where the time goes in v1:
time: 115 us
  Pallas kernels  103 us (90%)
  local copies, waits for them, and re-layouts  5.34 us (5%)
  between operations  2.47 us (2%)
  other arithmetic  1.98 us (2%)
  matrix products  1.81 us (2%)
    pallas_call x1, Pallas kernels, fused(): pl.pallas_call(functools.partial(fused_kernel, n), out_shape=(jax.ShapeDt...  103 us
    unnamed x9, local copies, waits for them, and re-layouts  5.27 us

profile of v1, /device:TPU:0, one launch (start us, length us, event | category | flops | bytes accessed | tf_op | source)
XLA Modules:
  0.0 114.6 jit_solution(4016756457260962700)
XLA Ops:
  0.6 0.0 copy-start
  0.7 0.1 pad.2.clone
  0.7 0.7 copy-done
  1.5 0.8 fusion.2
  2.3 1.0 fusion
  3.3 0.7 maximum_maximum_fusion.gs_in
  4.0 103.0 %shard_map.111 = (bf16[2048,512]{1,0:T(8,128)(2,1)}, f32[32,2048]{1,0:T(8,128)}, f32[128,512]{1,0:T(8,128)}, f32[8,128]{1,0:T(8,128)}) custom-call(f32[8,512]{1,0:T(8,128)} %maximum_maximum_fusion.gs_in, bf16[2048,512]{1,0:T(8,128)(2,1)} %bitcast.15, f32[1,2048]{1,0:T(1,128)} %bitcast.17, bf16[32,2048]{1,0:T(8,128)(2,1)} %w_in.1, bf16[128,512]{1,0:T(8,128)(2,1)} %w_out.1, ...), custom_call_target="tpu_custom_call" | custom-call | tf_op jit(solution)/shard_map/pallas_call | solution.py:446
  107.0 1.3 %reduce_sum.9 = f32[]{:T(128)} reduce(f32[8,128]{1,0:T(8,128)} %get-tuple-element.11, f32[]{:T(128)} %constant.1.clone.1), dimensions={0,1}, to_apply=%region_0.0 | reduce | flops 1023 | bytes 4104 | tf_op jit(solution)/shard_map/reduce_sum | solution.py:507
  108.9 0.0 copy-start.2
  108.9 0.0 copy-start.1
  108.9 3.1 %copy.15 = bf16[1,2048,512]{2,1,0:T(8,128)(2,1)} copy(bf16[1,2048,512]{2,1,0:T(8,128)(2,1)} %bitcast.16) | data formatting | bytes 4194304
  112.0 0.0 copy-done.2
  112.0 0.7 copy.16
  112.7 0.0 copy-done.1
  112.7 0.7 copy.17
  (2 shorter events, 0.0 us)
Async XLA Ops:
  0.6 0.8 copy-start
  108.9 3.1 %copy-start.2 = (f32[32,2048]{1,0:T(8,128)S(1)}, f32[32,2048]{1,0:T(8,128)}, u32[]{:S(2)}) copy-start(f32[32,2048]{1,0:T(8,128)} %get-tuple-element.17) | copy-start | bytes 786436
  108.9 3.8 %copy-start.1 = (f32[128,512]{1,0:T(8,128)S(1)}, f32[128,512]{1,0:T(8,128)}, u32[]{:S(2)}) copy-start(f32[128,512]{1,0:T(8,128)} %get-tuple-element.18) | copy-start | bytes 786436

commit v2 on v1

--- a/solution.py
+++ b/solution.py
@@ -118,9 +118,9 @@
 
 
 def fused_kernel(
-    n, gs_in, lat, b_in, w_in, w_out, target,
+    n, noise, cond_gain, cond_shift, lat, b_in, w_in, w_out, target,
     pred, gin, gout, crps,
-    win_s, wout_s, x_s, t_s, gs_s, p_s, norm_t, norm_s, act_s, slope_s, dp_s, dp_t, dpre_s, cr_s,
+    win_s, wout_s, x_s, t_s, gs_in, gs_s, p_s, norm_t, norm_s, act_s, slope_s, dp_s, dp_t, dpre_s, cr_s,
     pair_tx, pair_rx, ring_tx, ring_rx, mine_s, gin_tx, gout_tx, gin_rx, gout_rx, cr_tx, cr_rx,
     g_send, g_recv, q_send, q_recv, l_send, l_recv, local_sem, p_send, p_recv, o_sem,
     pair_ss, pair_rs, ring_ss, ring_rs, fin_ss, fin_rs, out_ss, out_rs, cr_ss, cr_rs,
@@ -141,7 +141,9 @@
     def place(offset):
         return (position + turn * offset + 2 * chips) % chips
 
-    following = (m, 2 * chip_at(place(1)) + core)
+    neighbours = ((m, 2 * chip_at(place(1)) + core), (m, 2 * chip_at(place(-1)) + core))
+    hops = (chips // 2, chips - 1 - chips // 2)
+    signs = (1, -1)
     twin = (m, 2 * chip + 1 - core)
     partner = (1 - m, f)
     flat = m * n + f
@@ -156,6 +158,10 @@
     def greet(k):
         pl.semaphore_signal(barrier, inc=1, device_id=device((flat + k) % total), device_id_type=MESH)
 
+    line = jnp.broadcast_to(noise[...], (8, noise.shape[1]))
+    for at, (base, table) in enumerate(((1.0, cond_gain), (0.0, cond_shift))):
+        product = jnp.dot(line, table[...], precision=lax.Precision.HIGHEST, preferred_element_type=jnp.float32)
+        gs_in[at] = base + product
     pl.semaphore_wait(barrier, total - 1)
 
     def remote(src, dst, send, recv, to):
@@ -176,21 +182,24 @@
             return win_s.at[pl.ds(pl.multiple_of(owner * rin, rin), rin)]
         return wout_s.at[pl.ds(pl.multiple_of(owner * rout, rout), rout)]
 
-    def ring_copy(which, step, src, owner):
-        return remote(src, slot(which, owner), g_send.at[which, step], g_recv.at[which, step], following)
-
-    def pair_copy(which, step, src, owner):
-        return remote(src, slot(which, owner), q_send.at[which, step], q_recv.at[which, step], twin)
+    def ring_copy(which, way, step, src, owner):
+        return remote(
+            src, slot(which, owner), g_send.at[which, way, step], g_recv.at[which, way, step], neighbours[way]
+        )
+
+    def pair_copy(which, way, step, src, owner):
+        return remote(src, slot(which, owner), q_send.at[which, way, step], q_recv.at[which, way, step], twin)
 
     shards = (w_in, w_out)
     for which in range(2):
-        ring_copy(which, 0, shards[which], f).start()
+        for way in range(2):
+            ring_copy(which, way, 0, shards[which], f).start()
     swap = remote(lat.at[pl.ds(other_from, half)], x_s.at[0], l_send.at[0], l_recv.at[0], partner)
     swap.start()
     gs_swap = remote(gs_in, gs_s.at[0], l_send.at[1], l_recv.at[1], partner)
     gs_swap.start()
     for which in range(2):
-        pair_copy(which, 0, shards[which], f).start()
+        pair_copy(which, 0, 0, shards[which], f).start()
     keep = pltpu.make_async_copy(lat.at[pl.ds(mine_from, half)], x_s.at[1], local_sem.at[0])
     keep.start()
     goal = pltpu.make_async_copy(target.at[pl.ds(mine_from, half)], t_s, local_sem.at[1])
@@ -200,24 +209,34 @@
     win_s[pl.ds(pl.multiple_of(f * rin, rin), rin), :] = w_in[...]
     wout_s[pl.ds(pl.multiple_of(f * rout, rout), rout), :] = w_out[...]
 
-    for step in range(1, chips):
-        owner = 2 * chip_at(place(-step)) + core
+    passed = []
+    for step in range(1, hops[0] + 1):
         for which in range(2):
-            ring_copy(which, step - 1, slot(which, owner), owner).wait_recv()
-            if step < chips - 1:
-                ring_copy(which, step, slot(which, owner), owner).start()
-            pair_copy(which, step, slot(which, owner), owner).start()
-    for step in range(chips):
-        owner = 2 * chip_at(place(step)) + 1 - core
-        for which in range(2):
-            pair_copy(which, step, slot(which, owner), owner).wait_recv()
-    for step in range(chips):
-        owner = 2 * chip_at(place(-step)) + core
-        for which in range(2):
-            src = shards[which] if step == 0 else slot(which, owner)
-            if step < chips - 1:
-                ring_copy(which, step, src, owner).wait_send()
-            pair_copy(which, step, src, owner).wait_send()
+            for way in range(2):
+                if step > hops[way]:
+                    continue
+                owner = 2 * chip_at(place(-signs[way] * step)) + core
+                here = slot(which, owner)
+                ring_copy(which, way, step - 1, here, owner).wait_recv()
+                if step < hops[way]:
+                    onward = ring_copy(which, way, step, here, owner)
+                    onward.start()
+                    passed.append(onward)
+                share = pair_copy(which, way, step, here, owner)
+                share.start()
+                passed.append(share)
+    for which in range(2):
+        pair_copy(which, 0, 0, shards[which], 2 * chip + 1 - core).wait_recv()
+        for way in range(2):
+            for step in range(1, hops[way] + 1):
+                owner = 2 * chip_at(place(signs[way] * step)) + 1 - core
+                pair_copy(which, way, step, slot(which, owner), owner).wait_recv()
+    for which in range(2):
+        for way in range(2):
+            passed.append(ring_copy(which, way, 0, shards[which], f))
+        passed.append(pair_copy(which, 0, 0, shards[which], f))
+    for sent in passed:
+        sent.wait_send()
     keep.wait()
     goal.wait()
     gs_swap.wait()
@@ -248,7 +267,7 @@
             center = jnp.mean(values, axis=1, keepdims=True)
             moved = values - center
             spread = jnp.mean(moved * moved, axis=1, keepdims=True)
-            normed = moved * lax.rsqrt(spread + 0.25) * gs_s[side, 0:1, :] + gs_s[side, 1:2, :]
+            normed = moved * lax.rsqrt(spread + 0.25) * gs_s[side, 0, 0:1, :] + gs_s[side, 1, 0:1, :]
             normed = normed.astype(jnp.bfloat16)
             norm_s[side * TILE : (side + 1) * TILE, :] = normed
         norm_t[:, rows] = norm_s[...].T
@@ -304,48 +323,55 @@
     def columns(owner):
         return pl.ds(pl.multiple_of(owner * cw, cw), cw)
 
-    def pair_sum(which, step):
-        return remote(
-            pair_tx.at[step, which], pair_rx.at[step, which], pair_ss.at[step, which], pair_rs.at[step, which], twin
-        )
-
-    def ring_sum(which, step):
-        return remote(
-            ring_tx.at[step, which], ring_rx.at[step, which], ring_ss.at[step, which], ring_rs.at[step, which], following
-        )
+    def pair_sum(way, step, which):
+        at = (way, step, which)
+        return remote(pair_tx.at[at], pair_rx.at[at], pair_ss.at[at], pair_rs.at[at], twin)
+
+    def ring_sum(way, step, which):
+        at = (way, step, which)
+        return remote(ring_tx.at[at], ring_rx.at[at], ring_ss.at[at], ring_rs.at[at], neighbours[way])
+
+    stages = hops[0]
 
     def compute(step):
-        own = columns(2 * chip_at(place(-step - 1)) + core)
-        twins = columns(2 * chip_at(place(step + 1)) + 1 - core)
-        for which, (left, right) in enumerate(((norm_t, dpre_s), (dp_t, act_s))):
-            both = jnp.concatenate([right[:, own], right[:, twins]], axis=1)
-            product = jnp.dot(left[...], both, preferred_element_type=jnp.float32)
-            mine_s[step, which] = product[:, :cw]
-            pair_tx[step, which] = product[:, cw:].astype(jnp.bfloat16)
-        for which in range(2):
-            pair_sum(which, step).start()
+        for way in range(2):
+            away = signs[way] * (hops[way] - step)
+            own = columns(2 * chip_at(place(away)) + core)
+            twins = columns(2 * chip_at(place(-away)) + 1 - core)
+            for which, (left, right) in enumerate(((norm_t, dpre_s), (dp_t, act_s))):
+                both = jnp.concatenate([right[:, own], right[:, twins]], axis=1)
+                product = jnp.dot(left[...], both, preferred_element_type=jnp.float32)
+                mine_s[way, step, which] = product[:, :cw]
+                pair_tx[way, step, which] = product[:, cw:].astype(jnp.bfloat16)
+        for way in range(2):
+            for which in range(2):
+                pair_sum(way, step, which).start()
 
     def finish(step, first=False, last=False):
-        for which in range(2):
-            pair_sum(which, step).wait_recv()
-            value = mine_s[step, which] + pair_rx[step, which].astype(jnp.float32)
-            if not first:
-                ring_sum(which, step - 1).wait_recv()
-                value = value + ring_rx[step - 1, which].astype(jnp.float32)
-            value = value.astype(jnp.bfloat16)
-            if not last:
-                ring_tx[step, which] = value
-                ring_sum(which, step).start()
-            elif which == 0:
-                gin_tx[...] = value
-            else:
-                gout_tx[...] = value
+        for way in range(2):
+            for which in range(2):
+                pair_sum(way, step, which).wait_recv()
+                value = mine_s[way, step, which] + pair_rx[way, step, which].astype(jnp.float32)
+                if not first:
+                    ring_sum(way, step - 1, which).wait_recv()
+                    value = value + ring_rx[way, step - 1, which].astype(jnp.float32)
+                if last and way == 1:
+                    ring_sum(0, step, which).wait_recv()
+                    value = value + ring_rx[0, step, which].astype(jnp.float32)
+                value = value.astype(jnp.bfloat16)
+                if not last or way == 0:
+                    ring_tx[way, step, which] = value
+                    ring_sum(way, step, which).start()
+                elif which == 0:
+                    gin_tx[...] = value
+                else:
+                    gout_tx[...] = value
 
     compute(0)
     compute(1)
     finish(0, first=True)
 
-    @pl.loop(1, chips - 1)
+    @pl.loop(1, stages - 1)
     def steps(step):
         compute(step + 1)
         finish(step)
@@ -354,7 +380,7 @@
     def tell(k):
         cr_copy((flat + k) % total, flat).start()
 
-    finish(chips - 1, last=True)
+    finish(stages - 1, last=True)
 
     def fin_copy(to, source):
         target_rows = pl.ds(pl.multiple_of((to % n) * rin, rin), rin)
@@ -373,7 +399,7 @@
     def heard(k):
         cr_copy(flat, (flat + k) % total).wait_recv()
 
-    crps[...] = jnp.sum(cr_rx[...], axis=0)
+    crps[0, 0] = jnp.sum(jnp.sum(cr_rx[...], axis=0)) / jnp.float32(4 * n * half * width)
 
     out_copy.wait_recv()
     gout[...] = (gout_tx[...].astype(jnp.float32) + gout_rx[...].astype(jnp.float32)).T
@@ -392,15 +418,18 @@
         here.wait()
         arrival(tile).wait_recv()
 
-    @pl.loop(0, chips - 1)
-    def settle_ring(step):
-        for which in range(2):
-            ring_sum(which, step).wait_send()
-
-    @pl.loop(0, chips)
+    @pl.loop(0, stages)
     def settle_pair(step):
-        for which in range(2):
-            pair_sum(which, step).wait_send()
+        for way in range(2):
+            for which in range(2):
+                pair_sum(way, step, which).wait_send()
+
+    for way in range(2):
+
+        @pl.loop(0, hops[way])
+        def settle_ring(step):
+            for which in range(2):
+                ring_sum(way, step, which).wait_send()
 
     out_copy.wait_send()
 
@@ -436,9 +465,8 @@
     chips = n // 2
     tiles = half // TILE
     cw = hidden // n
+    stages = chips // 2
     rin, rout = w_in.shape[0], w_out.shape[0]
-    exact = functools.partial(jnp.dot, precision=lax.Precision.HIGHEST, preferred_element_type=jnp.float32)
-    gs = jnp.concatenate([1.0 + exact(noise, cond_gain), exact(noise, cond_shift), jnp.zeros((6, width), jnp.float32)])
     bf, f32 = jnp.bfloat16, jnp.float32
     vmem = pl.BlockSpec(memory_space=pltpu.VMEM)
     anywhere = pl.BlockSpec(memory_space=pl.ANY)
@@ -449,16 +477,17 @@
             jax.ShapeDtypeStruct((rows, width), bf),
             jax.ShapeDtypeStruct((rin, hidden), f32),
             jax.ShapeDtypeStruct((rout, width), f32),
-            jax.ShapeDtypeStruct((8, 128), f32),
+            jax.ShapeDtypeStruct((1, 1), f32),
         ),
-        in_specs=[vmem, anywhere, vmem, vmem, vmem, anywhere],
-        out_specs=(anywhere, vmem, vmem, vmem),
+        in_specs=[vmem, vmem, vmem, anywhere, vmem, vmem, vmem, anywhere],
+        out_specs=(anywhere, vmem, vmem, pl.BlockSpec(memory_space=pltpu.SMEM)),
         scratch_shapes=[
             pltpu.VMEM((width, hidden), bf),
             pltpu.VMEM((hidden, width), bf),
             pltpu.VMEM((2, half, width), bf),
             pltpu.VMEM((half, width), bf),
             pltpu.VMEM((2, 8, width), f32),
+            pltpu.VMEM((2, 2, 8, width), f32),
             pltpu.VMEM((2, half, width), bf),
             pltpu.VMEM((width, rows), bf),
             pltpu.VMEM((2 * TILE, width), bf),
@@ -468,31 +497,31 @@
             pltpu.VMEM((width, rows), bf),
             pltpu.VMEM((rows, hidden), bf),
             pltpu.VMEM((8, width), f32),
-            pltpu.VMEM((chips, 2, width, cw), bf),
-            pltpu.VMEM((chips, 2, width, cw), bf),
-            pltpu.VMEM((chips - 1, 2, width, cw), bf),
-            pltpu.VMEM((chips - 1, 2, width, cw), bf),
-            pltpu.VMEM((chips, 2, width, cw), f32),
+            pltpu.VMEM((2, stages, 2, width, cw), bf),
+            pltpu.VMEM((2, stages, 2, width, cw), bf),
+            pltpu.VMEM((2, stages, 2, width, cw), bf),
+            pltpu.VMEM((2, stages, 2, width, cw), bf),
+            pltpu.VMEM((2, stages, 2, width, cw), f32),
             pltpu.VMEM((width, cw), bf),
             pltpu.VMEM((width, cw), bf),
             pltpu.VMEM((2 * n, rin, cw), bf),
             pltpu.VMEM((width, cw), bf),
             pltpu.VMEM((8, 128), f32),
             pltpu.VMEM((2 * n, 8, 128), f32),
-            dma((2, chips)),
-            dma((2, chips)),
-            dma((2, chips)),
-            dma((2, chips)),
+            dma((2, 2, stages + 1)),
+            dma((2, 2, stages + 1)),
+            dma((2, 2, stages + 1)),
+            dma((2, 2, stages + 1)),
             dma((2,)),
             dma((2,)),
             dma((2,)),
             dma((tiles,)),
             dma((tiles,)),
             dma((tiles,)),
-            dma((chips, 2)),
-            dma((chips, 2)),
-            dma((chips, 2)),
-            dma((chips, 2)),
+            dma((2, stages, 2)),
+            dma((2, stages, 2)),
+            dma((2, stages, 2)),
+            dma((2, stages, 2)),
             dma((2 * n,)),
             dma((2 * n,)),
             dma,
@@ -503,8 +532,8 @@
         compiler_params=pltpu.CompilerParams(
             collective_id=0, has_side_effects=True, vmem_limit_bytes=60 * 1024 * 1024
         ),
-    )(gs, block, b_in[None, :], w_in, w_out, target)
-    crps_mean = jnp.sum(parts) / jnp.float32(2 * rows * n * width)
+    )(noise, cond_gain, cond_shift, block, b_in[None, :], w_in, w_out, target)
+    crps_mean = parts.reshape(())
     return (prediction[None], grad_in, grad_out, crps_mean)
 
 

time: 115 us -> 102 us (0.89)
  Pallas kernels: 103 us -> 94.4 us
  other arithmetic: 1.98 us -> 0 us
  matrix products: 1.81 us -> 0 us
    pallas_call x1, Pallas kernels: 103 us -> 94.4 us  [fused(): pl.pallas_call(functools.partial(fused_kernel, n), out_shape=(jax.ShapeDt...]
    dot_general x2 -> x0, matrix products: 1.81 us -> none  [the longest x1 1.01 us: fused(): exact(noise, cond_shift)]
    reduce_sum x1 -> x0, other arithmetic: 1.29 us -> none  [fused(): crps_mean = jnp.sum(parts) / jnp.float32(2 * rows * n * width)]
    unnamed x9 -> x7, local copies, waits for them, and re-layouts: 5.27 us -> 4.51 us
where the time goes in v2:
time: 102 us; the launch traced here: 101 us
  Pallas kernels  94.4 us (93%)
  local copies, waits for them, and re-layouts  4.51 us (4%)
  between operations  2.46 us (2%)
    pallas_call x1, Pallas kernels, fused(): pl.pallas_call(functools.partial(fused_kernel, n), out_shape=(jax.ShapeDt...  94.4 us
    unnamed x7, local copies, waits for them, and re-layouts  4.51 us

profile of v2, /device:TPU:0, one launch (start us, length us, event | category | flops | bytes accessed | tf_op | source)
XLA Modules:
  0.0 101.4 jit_solution(2437090022056850248)
XLA Ops:
  0.6 94.4 %shard_map.111 = (bf16[2048,512]{1,0:T(8,128)(2,1)}, f32[32,2048]{1,0:T(8,128)}, f32[128,512]{1,0:T(8,128)}, f32[1,1]{1,0:T(1,128)}) custom-call(f32[1,32]{1,0:T(1,128)} %noise.1, f32[32,512]{1,0:T(8,128)} %cond_gain.1, f32[32,512]{1,0:T(8,128)} %cond_shift.1, bf16[2048,512]{1,0:T(8,128)(2,1)} %bitcast.4, f32[1,2048]{1,0:T(1,128)} %bitcast.6, ...), custom_call_target="tpu_custom_call" | custom-call | tf_op jit(solution)/shard_map/pallas_call | solution.py:474
  95.0 0.0 copy-start.1
  95.1 0.0 copy-start
  95.1 3.1 %copy.16 = bf16[1,2048,512]{2,1,0:T(8,128)(2,1)} copy(bf16[1,2048,512]{2,1,0:T(8,128)(2,1)} %bitcast.5) | data formatting | bytes 4194304
  98.2 0.0 copy-done.1
  98.2 0.7 copy.17
  98.9 0.0 copy-done
  98.9 0.7 copy.18
Async XLA Ops:
  95.0 3.1 %copy-start.1 = (f32[32,2048]{1,0:T(8,128)S(1)}, f32[32,2048]{1,0:T(8,128)}, u32[]{:S(2)}) copy-start(f32[32,2048]{1,0:T(8,128)} %get-tuple-element.17) | copy-start | bytes 786436
  95.1 3.8 %copy-start = (f32[128,512]{1,0:T(8,128)S(1)}, f32[128,512]{1,0:T(8,128)}, u32[]{:S(2)}) copy-start(f32[128,512]{1,0:T(8,128)} %get-tuple-element.18) | copy-start | bytes 786436

commit v3 on v2

--- a/solution.py
+++ b/solution.py
@@ -120,7 +120,7 @@
 def fused_kernel(
     n, noise, cond_gain, cond_shift, lat, b_in, w_in, w_out, target,
     pred, gin, gout, crps,
-    win_s, wout_s, x_s, t_s, gs_in, gs_s, p_s, norm_t, norm_s, act_s, slope_s, dp_s, dp_t, dpre_s, cr_s,
+    win_s, wout_s, x_s, t_s, gs_in, gs_s, p_s, norm_t, norm_s, act_s, dp_s, dp_t, dpre_s, cr_s,
     pair_tx, pair_rx, ring_tx, ring_rx, mine_s, gin_tx, gout_tx, gin_rx, gout_rx, cr_tx, cr_rx,
     g_send, g_recv, q_send, q_recv, l_send, l_recv, local_sem, p_send, p_recv, o_sem,
     pair_ss, pair_rs, ring_ss, ring_rs, fin_ss, fin_rs, out_ss, out_rs, cr_ss, cr_rs,
@@ -210,66 +210,35 @@
     wout_s[pl.ds(pl.multiple_of(f * rout, rout), rout), :] = w_out[...]
 
     passed = []
-    for step in range(1, hops[0] + 1):
-        for which in range(2):
-            for way in range(2):
-                if step > hops[way]:
-                    continue
-                owner = 2 * chip_at(place(-signs[way] * step)) + core
-                here = slot(which, owner)
-                ring_copy(which, way, step - 1, here, owner).wait_recv()
-                if step < hops[way]:
-                    onward = ring_copy(which, way, step, here, owner)
-                    onward.start()
-                    passed.append(onward)
-                share = pair_copy(which, way, step, here, owner)
-                share.start()
-                passed.append(share)
-    for which in range(2):
+
+    def forward(which, way, step):
+        owner = 2 * chip_at(place(-signs[way] * step)) + core
+        here = slot(which, owner)
+        ring_copy(which, way, step - 1, here, owner).wait_recv()
+        if step < hops[way]:
+            onward = ring_copy(which, way, step, here, owner)
+            onward.start()
+            passed.append(onward)
+        share = pair_copy(which, way, step, here, owner)
+        share.start()
+        passed.append(share)
+
+    def shared(which):
         pair_copy(which, 0, 0, shards[which], 2 * chip + 1 - core).wait_recv()
         for way in range(2):
             for step in range(1, hops[way] + 1):
                 owner = 2 * chip_at(place(signs[way] * step)) + 1 - core
                 pair_copy(which, way, step, slot(which, owner), owner).wait_recv()
-    for which in range(2):
-        for way in range(2):
-            passed.append(ring_copy(which, way, 0, shards[which], f))
-        passed.append(pair_copy(which, 0, 0, shards[which], f))
-    for sent in passed:
-        sent.wait_send()
-    keep.wait()
-    goal.wait()
-    gs_swap.wait()
-    swap.wait()
-
-    tiles = half // TILE
-    scale = (1.0 / (2.0 * n * 2 * half) ** 0.5)
-
-    def home(tile):
-        start = pl.multiple_of(tile * TILE, TILE)
-        there = pl.multiple_of(m * half + tile * TILE, TILE)
-        back = remote(p_s.at[0, pl.ds(start, TILE)], pred.at[pl.ds(there, TILE)], p_send.at[tile], p_recv.at[tile], partner)
-        here = pltpu.make_async_copy(p_s.at[1, pl.ds(start, TILE)], pred.at[pl.ds(there, TILE)], o_sem.at[tile])
-        return back, here
-
-    def arrival(tile):
-        start = pl.multiple_of(tile * TILE, TILE)
-        there = pl.multiple_of((1 - m) * half + tile * TILE, TILE)
-        return remote(p_s.at[0, pl.ds(start, TILE)], pred.at[pl.ds(there, TILE)], p_send.at[tile], p_recv.at[tile], partner)
-
-    @pl.loop(0, tiles)
-    def nodes(tile):
-        start = pl.multiple_of(tile * TILE, TILE)
-        base = pl.multiple_of(tile * 2 * TILE, 2 * TILE)
-        rows = pl.ds(base, 2 * TILE)
-        for side in range(2):
-            values = x_s[side, pl.ds(start, TILE), :].astype(jnp.float32)
-            center = jnp.mean(values, axis=1, keepdims=True)
-            moved = values - center
-            spread = jnp.mean(moved * moved, axis=1, keepdims=True)
-            normed = moved * lax.rsqrt(spread + 0.25) * gs_s[side, 0, 0:1, :] + gs_s[side, 1, 0:1, :]
-            normed = normed.astype(jnp.bfloat16)
-            norm_s[side * TILE : (side + 1) * TILE, :] = normed
+
+    def hidden_units(side, tile):
+        start = pl.multiple_of(tile * WIDE, WIDE)
+        rows = pl.ds(pl.multiple_of(side * half + start, WIDE), WIDE)
+        values = x_s[side, pl.ds(start, WIDE), :].astype(jnp.float32)
+        center = jnp.mean(values, axis=1, keepdims=True)
+        moved = values - center
+        spread = jnp.mean(moved * moved, axis=1, keepdims=True)
+        normed = moved * lax.rsqrt(spread + 0.25) * gs_s[side, 0, 0:1, :] + gs_s[side, 1, 0:1, :]
+        norm_s[...] = normed.astype(jnp.bfloat16)
         norm_t[:, rows] = norm_s[...].T
         for j in range(hidden // WIDE):
             cols = slice(j * WIDE, (j + 1) * WIDE)
@@ -278,8 +247,59 @@
             u = jnp.tanh(COEF * (v + CUBIC * square * v))
             gate = 0.5 * (1.0 + u)
             act_s[rows, cols] = (v * gate).astype(jnp.bfloat16)
-            slope_s[:, cols] = gate + (0.5 * COEF) * v * (1.0 - u * u) * (1.0 + 3.0 * CUBIC * square)
-        out = jnp.dot(act_s[rows, :], wout_s[...], preferred_element_type=jnp.float32)
+            slope = gate + (0.5 * COEF) * v * (1.0 - u * u) * (1.0 + 3.0 * CUBIC * square)
+            dpre_s[rows, cols] = slope.astype(jnp.bfloat16)
+
+    for step in range(1, hops[0]):
+        for which in range(2):
+            for way in range(2):
+                forward(which, way, step)
+    forward(0, 0, hops[0])
+    keep.wait()
+    shared(0)
+
+    @pl.loop(0, half // WIDE)
+    def own_side(tile):
+        hidden_units(1, tile)
+
+    forward(1, 0, hops[0])
+    gs_swap.wait()
+    swap.wait()
+
+    @pl.loop(0, half // WIDE)
+    def other_side(tile):
+        hidden_units(0, tile)
+
+    shared(1)
+    for which in range(2):
+        for way in range(2):
+            passed.append(ring_copy(which, way, 0, shards[which], f))
+        passed.append(pair_copy(which, 0, 0, shards[which], f))
+    for sent in passed:
+        sent.wait_send()
+    goal.wait()
+
+    tiles = half // TILE
+    scale = (1.0 / (2.0 * n * 2 * half) ** 0.5)
+
+    def home(tile):
+        start = pl.multiple_of(tile * TILE, TILE)
+        there = pl.multiple_of(m * half + tile * TILE, TILE)
+        back = remote(p_s.at[0, pl.ds(start, TILE)], pred.at[pl.ds(there, TILE)], p_send.at[tile], p_recv.at[tile], partner)
+        here = pltpu.make_async_copy(p_s.at[1, pl.ds(start, TILE)], pred.at[pl.ds(there, TILE)], o_sem.at[tile])
+        return back, here
+
+    def arrival(tile):
+        start = pl.multiple_of(tile * TILE, TILE)
+        there = pl.multiple_of((1 - m) * half + tile * TILE, TILE)
+        return remote(p_s.at[0, pl.ds(start, TILE)], pred.at[pl.ds(there, TILE)], p_send.at[tile], p_recv.at[tile], partner)
+
+    @pl.loop(0, tiles)
+    def nodes(tile):
+        start = pl.multiple_of(tile * TILE, TILE)
+        parts = (pl.ds(start, TILE), pl.ds(pl.multiple_of(half + start, TILE), TILE))
+        acts = jnp.concatenate([act_s[rows, :] for rows in parts], axis=0)
+        out = jnp.dot(acts, wout_s[...], preferred_element_type=jnp.float32)
         guess = []
         for side in range(2):
             value = x_s[side, pl.ds(start, TILE), :].astype(jnp.float32) + out[side * TILE : (side + 1) * TILE]
@@ -298,13 +318,17 @@
         cr_s[...] += jnp.sum(value_sum.reshape(TILE // 8, 8, width), axis=0)
         dp_s[:TILE, :] = ((slopes[0] - slopes[2]) * scale).astype(jnp.bfloat16)
         dp_s[TILE:, :] = ((slopes[1] + slopes[2]) * scale).astype(jnp.bfloat16)
-        dp_t[:, rows] = dp_s[...].T
+        turned = dp_s[...].T
+        for side, rows in enumerate(parts):
+            dp_t[:, rows] = turned[:, side * TILE : (side + 1) * TILE]
         for j in range(hidden // WIDE):
             cols = slice(j * WIDE, (j + 1) * WIDE)
             dact = lax.dot_general(
                 dp_s[...], wout_s[cols, :], (((1,), (1,)), ((), ())), preferred_element_type=jnp.float32
             )
-            dpre_s[rows, cols] = (dact * slope_s[:, cols]).astype(jnp.bfloat16)
+            for side, rows in enumerate(parts):
+                piece = dact[side * TILE : (side + 1) * TILE] * dpre_s[rows, cols].astype(jnp.float32)
+                dpre_s[rows, cols] = piece.astype(jnp.bfloat16)
         back, here = home(tile)
         back.start()
         here.start()
@@ -322,6 +346,12 @@
 
     def columns(owner):
         return pl.ds(pl.multiple_of(owner * cw, cw), cw)
+
+    def fin_copy(to, source):
+        target_rows = pl.ds(pl.multiple_of((to % n) * rin, rin), rin)
+        return remote(gin_tx.at[target_rows], gin_rx.at[source], fin_ss.at[to], fin_rs.at[source], device(to))
+
+    out_copy = remote(gout_tx, gout_rx, out_ss, out_rs, partner)
 
     def pair_sum(way, step, which):
         at = (way, step, which)
@@ -364,8 +394,14 @@
                     ring_sum(way, step, which).start()
                 elif which == 0:
                     gin_tx[...] = value
+
+                    @pl.loop(1, total)
+                    def scatter(k):
+                        fin_copy((flat + k) % total, flat).start()
+
                 else:
                     gout_tx[...] = value
+                    out_copy.start()
 
     compute(0)
     compute(1)
@@ -381,17 +417,6 @@
         cr_copy((flat + k) % total, flat).start()
 
     finish(stages - 1, last=True)
-
-    def fin_copy(to, source):
-        target_rows = pl.ds(pl.multiple_of((to % n) * rin, rin), rin)
-        return remote(gin_tx.at[target_rows], gin_rx.at[source], fin_ss.at[to], fin_rs.at[source], device(to))
-
-    out_copy = remote(gout_tx, gout_rx, out_ss, out_rs, partner)
-    out_copy.start()
-
-    @pl.loop(1, total)
-    def scatter(k):
-        fin_copy((flat + k) % total, flat).start()
 
     gin_rx[flat] = gin_tx[pl.ds(pl.multiple_of(f * rin, rin), rin), :]
 
@@ -450,7 +475,7 @@
         and (width // n) % 16 == 0
         and width % 128 == 0
         and hidden % WIDE == 0
-        and rows % (2 * TILE) == 0
+        and rows % (2 * WIDE) == 0
         and rows * hidden <= 2048 * 2048
         and width * hidden <= 512 * 2048
     )
@@ -490,9 +515,8 @@
             pltpu.VMEM((2, 2, 8, width), f32),
             pltpu.VMEM((2, half, width), bf),
             pltpu.VMEM((width, rows), bf),
-            pltpu.VMEM((2 * TILE, width), bf),
+            pltpu.VMEM((WIDE, width), bf),
             pltpu.VMEM((rows, hidden), bf),
-            pltpu.VMEM((2 * TILE, hidden), f32),
             pltpu.VMEM((2 * TILE, width), bf),
             pltpu.VMEM((width, rows), bf),
             pltpu.VMEM((rows, hidden), bf),

time: 102 us -> 103 us (level)
  Pallas kernels: 94.4 us -> 95.9 us
    pallas_call x1, Pallas kernels: 94.4 us -> 95.9 us  [fused(): pl.pallas_call(functools.partial(fused_kernel, n), out_shape=(jax.ShapeDt...]
where the time goes in v3:
time: 103 us
  Pallas kernels  95.9 us (93%)
  local copies, waits for them, and re-layouts  4.51 us (4%)
  between operations  2.46 us (2%)
    pallas_call x1, Pallas kernels, fused(): pl.pallas_call(functools.partial(fused_kernel, n), out_shape=(jax.ShapeDt...  95.9 us
    unnamed x7, local copies, waits for them, and re-layouts  4.51 us

profile of v3, /device:TPU:0, one launch (start us, length us, event | category | flops | bytes accessed | tf_op | source)
XLA Modules:
  0.0 102.9 jit_solution(18085011361156123972)
XLA Ops:
  0.6 95.9 %shard_map.111 = (bf16[2048,512]{1,0:T(8,128)(2,1)}, f32[32,2048]{1,0:T(8,128)}, f32[128,512]{1,0:T(8,128)}, f32[1,1]{1,0:T(1,128)}) custom-call(f32[1,32]{1,0:T(1,128)} %noise.1, f32[32,512]{1,0:T(8,128)} %cond_gain.1, f32[32,512]{1,0:T(8,128)} %cond_shift.1, bf16[2048,512]{1,0:T(8,128)(2,1)} %bitcast.4, f32[1,2048]{1,0:T(1,128)} %bitcast.6, ...), custom_call_target="tpu_custom_call" | custom-call | tf_op jit(solution)/shard_map/pallas_call | solution.py:499
  96.5 0.0 copy-start.1
  96.6 0.0 copy-start
  96.6 3.1 %copy.16 = bf16[1,2048,512]{2,1,0:T(8,128)(2,1)} copy(bf16[1,2048,512]{2,1,0:T(8,128)(2,1)} %bitcast.5) | data formatting | bytes 4194304
  99.7 0.0 copy-done.1
  99.7 0.7 copy.17
  100.4 0.0 copy-done
  100.4 0.7 copy.18
Async XLA Ops:
  96.5 3.1 %copy-start.1 = (f32[32,2048]{1,0:T(8,128)S(1)}, f32[32,2048]{1,0:T(8,128)}, u32[]{:S(2)}) copy-start(f32[32,2048]{1,0:T(8,128)} %get-tuple-element.17) | copy-start | bytes 786436
  96.6 3.8 %copy-start = (f32[128,512]{1,0:T(8,128)S(1)}, f32[128,512]{1,0:T(8,128)}, u32[]{:S(2)}) copy-start(f32[128,512]{1,0:T(8,128)} %get-tuple-element.18) | copy-start | bytes 786436

commit v4 on v2

--- a/solution.py
+++ b/solution.py
@@ -323,6 +323,12 @@
     def columns(owner):
         return pl.ds(pl.multiple_of(owner * cw, cw), cw)
 
+    def fin_copy(to, source):
+        target_rows = pl.ds(pl.multiple_of((to % n) * rin, rin), rin)
+        return remote(gin_tx.at[target_rows], gin_rx.at[source], fin_ss.at[to], fin_rs.at[source], device(to))
+
+    out_copy = remote(gout_tx, gout_rx, out_ss, out_rs, partner)
+
     def pair_sum(way, step, which):
         at = (way, step, which)
         return remote(pair_tx.at[at], pair_rx.at[at], pair_ss.at[at], pair_rs.at[at], twin)
@@ -364,8 +370,14 @@
                     ring_sum(way, step, which).start()
                 elif which == 0:
                     gin_tx[...] = value
+
+                    @pl.loop(1, total)
+                    def scatter(k):
+                        fin_copy((flat + k) % total, flat).start()
+
                 else:
                     gout_tx[...] = value
+                    out_copy.start()
 
     compute(0)
     compute(1)
@@ -381,17 +393,6 @@
         cr_copy((flat + k) % total, flat).start()
 
     finish(stages - 1, last=True)
-
-    def fin_copy(to, source):
-        target_rows = pl.ds(pl.multiple_of((to % n) * rin, rin), rin)
-        return remote(gin_tx.at[target_rows], gin_rx.at[source], fin_ss.at[to], fin_rs.at[source], device(to))
-
-    out_copy = remote(gout_tx, gout_rx, out_ss, out_rs, partner)
-    out_copy.start()
-
-    @pl.loop(1, total)
-    def scatter(k):
-        fin_copy((flat + k) % total, flat).start()
 
     gin_rx[flat] = gin_tx[pl.ds(pl.multiple_of(f * rin, rin), rin), :]
 

time: 102 us -> 101 us (level)
  no operation moved by 1% of the time
where the time goes in v4:
time: 101 us
  Pallas kernels  93.9 us (93%)
  local copies, waits for them, and re-layouts  4.51 us (4%)
  between operations  2.46 us (2%)
    pallas_call x1, Pallas kernels, fused(): pl.pallas_call(functools.partial(fused_kernel, n), out_shape=(jax.ShapeDt...  93.9 us
    unnamed x7, local copies, waits for them, and re-layouts  4.51 us

profile of v4, /device:TPU:0, one launch (start us, length us, event | category | flops | bytes accessed | tf_op | source)
XLA Modules:
  0.0 100.8 jit_solution(1451291597956022179)
XLA Ops:
  0.6 93.9 %shard_map.111 = (bf16[2048,512]{1,0:T(8,128)(2,1)}, f32[32,2048]{1,0:T(8,128)}, f32[128,512]{1,0:T(8,128)}, f32[1,1]{1,0:T(1,128)}) custom-call(f32[1,32]{1,0:T(1,128)} %noise.1, f32[32,512]{1,0:T(8,128)} %cond_gain.1, f32[32,512]{1,0:T(8,128)} %cond_shift.1, bf16[2048,512]{1,0:T(8,128)(2,1)} %bitcast.4, f32[1,2048]{1,0:T(1,128)} %bitcast.6, ...), custom_call_target="tpu_custom_call" | custom-call | tf_op jit(solution)/shard_map/pallas_call | solution.py:475
  94.5 0.0 copy-start.1
  94.5 0.0 copy-start
  94.5 3.1 %copy.16 = bf16[1,2048,512]{2,1,0:T(8,128)(2,1)} copy(bf16[1,2048,512]{2,1,0:T(8,128)(2,1)} %bitcast.5) | data formatting | bytes 4194304
  97.6 0.0 copy-done.1
  97.6 0.7 copy.17
  98.3 0.0 copy-done
  98.3 0.7 copy.18
Async XLA Ops:
  94.5 3.1 %copy-start.1 = (f32[32,2048]{1,0:T(8,128)S(1)}, f32[32,2048]{1,0:T(8,128)}, u32[]{:S(2)}) copy-start(f32[32,2048]{1,0:T(8,128)} %get-tuple-element.17) | copy-start | bytes 786436
  94.5 3.8 %copy-start = (f32[128,512]{1,0:T(8,128)S(1)}, f32[128,512]{1,0:T(8,128)}, u32[]{:S(2)}) copy-start(f32[128,512]{1,0:T(8,128)} %get-tuple-element.18) | copy-start | bytes 786436
